TPU v7x, 32 devices: a whole 2x2x4 slice. The times are simulated.
32 devices in a mesh: dp: 4 (over x, core), seq: 8 (over z, y).
Axes of the slice: x: 2, y: 2, z: 4, core: 2. Of those that a mesh axis runs over, the one named last changes fastest.
Arguments:
- block_input: bfloat16 [16384, 2560], P(('dp', 'seq')), may hold values from -6 to 6
- w_query: bfloat16 [2560, 2560], P('dp', 'seq'), may hold values from -4 to 4
- w_keyval: bfloat16 [2560, 512], P('dp', 'seq'), may hold values from -0.125 to 0.125
- w_out: bfloat16 [2560, 2560], P('dp', 'seq'), may hold values from -2 to 2
- gain_attn: bfloat16 [2560], P(('dp', 'seq')), may hold values from 0.5 to 1.5
- w_gate: bfloat16 [2560, 7680], P('dp', 'seq'), may hold values from -0.125 to 0.125
- w_up: bfloat16 [2560, 7680], P('dp', 'seq'), may hold values from -0.125 to 0.125
- w_down: bfloat16 [2560, 7680], P('dp', 'seq'), may hold values from -0.0625 to 0.0625
- gain_mlp: bfloat16 [2560], P(('dp', 'seq')), may hold values from 0.5 to 1.5
- cotangent: bfloat16 [16384, 2560], P(('dp', 'seq')), may hold values from -6 to 6
Outputs:
- output_rows: bfloat16 [16384, 2560], P(('dp', 'seq'))
- grad_input: float32 [16384, 2560], P(('dp', 'seq'))
- grad_w_query: float32 [2560, 2560], P('dp', 'seq')
- grad_w_keyval: float32 [2560, 512], P('dp', 'seq')
- grad_w_out: float32 [2560, 2560], P('dp', 'seq')
- grad_gain_attn: float32 [2560], P(('dp', 'seq'))
- grad_w_gate: float32 [2560, 7680], P('dp', 'seq')
- grad_w_up: float32 [2560, 7680], P('dp', 'seq')
- grad_w_down: float32 [2560, 7680], P('dp', 'seq')
- grad_gain_mlp: float32 [2560], P(('dp', 'seq'))
All inputs are finite; a program needn't handle non-finite values.
Results may differ from a plain program's by a relative error of at most 0.019.
The roundings to bfloat16 on the way count: a program that leaves them out, or rounds other values in their place, can miss the bound.
Values may be sent and summed in bfloat16 or wider, within the bound.
A program may use at most 576 MiB of HBM per device.

v0:
```python
import jax
import jax.numpy as jnp
from jax import lax
from jax.sharding import PartitionSpec as P

HEADS = 10
HD = 256
WINDOW = 2048


def shifted(shard, axis, by):
    length = lax.axis_size(axis)
    pairs = [(i, i + by) for i in range(length) if 0 <= i + by < length]
    return lax.ppermute(shard, axis, pairs)


def norm_rows(values, gain):
    return values * lax.rsqrt(jnp.mean(values * values, axis=-1, keepdims=True) + 1e-06) * gain


def rotate(values, positions):
    rope_width = values.shape[-1] // 2
    half_width = rope_width // 2
    frequency = 10000.0 ** (-jnp.arange(half_width, dtype=jnp.float32) / half_width)
    angles = positions.astype(jnp.float32)[:, None] * frequency[None, :]
    cosine = jnp.cos(angles)
    sine_part = jnp.sin(angles)
    first_half = values[..., :half_width]
    second_half = values[..., half_width:rope_width]
    unturned = values[..., rope_width:]
    return jnp.concatenate(
        [
            first_half * cosine - second_half * sine_part,
            second_half * cosine + first_half * sine_part,
            unturned,
        ],
        axis=-1,
    )


def gelu_tanh(v):
    return jax.nn.gelu(v, approximate=True)


def contract_rows(left, right):
    return lax.dot_general(
        left, right, (((0,), (0,)), ((), ())), preferred_element_type=jnp.float32
    )


def contract_last(left, right):
    return lax.dot_general(
        left, right, (((1,), (1,)), ((), ())), preferred_element_type=jnp.float32
    )


def local(
    block_input, w_query, w_keyval, w_out, gain_attn, w_gate, w_up, w_down, gain_mlp, cotangent
):
    row_count = block_input.shape[0]
    seq_size = lax.axis_size("seq")
    seq_place = lax.axis_index("seq")
    depth = min((WINDOW + row_count - 2) // row_count, seq_size - 1)
    score_scale = HD ** (-0.5)
    positions = seq_place * row_count + jnp.arange(row_count, dtype=jnp.int32)
    column_part = (
        lax.all_gather(w_query, "seq", axis=1, tiled=True),
        lax.all_gather(w_keyval, "seq", axis=1, tiled=True),
        lax.all_gather(w_out, "seq", axis=1, tiled=True),
        lax.all_gather(w_gate, "seq", axis=1, tiled=True),
        lax.all_gather(w_up, "seq", axis=1, tiled=True),
        lax.all_gather(w_down, "seq", axis=1, tiled=True),
        lax.all_gather(gain_attn, "seq", axis=0, tiled=True),
        lax.all_gather(gain_mlp, "seq", axis=0, tiled=True),
    )
    query_full, keyval_full, out_full, gate_full, up_full, down_full, gain_one, gain_two = (
        lax.all_gather(column_part[0], "dp", axis=0, tiled=True),
        lax.all_gather(column_part[1], "dp", axis=0, tiled=True),
        lax.all_gather(column_part[2], "dp", axis=0, tiled=True),
        lax.all_gather(column_part[3], "dp", axis=0, tiled=True),
        lax.all_gather(column_part[4], "dp", axis=0, tiled=True),
        lax.all_gather(column_part[5], "dp", axis=0, tiled=True),
        lax.all_gather(column_part[6], "dp", axis=0, tiled=True),
        lax.all_gather(column_part[7], "dp", axis=0, tiled=True),
    )
    inputs = block_input.astype(jnp.float32)
    normed_one_f, norm_one_pull = jax.vjp(norm_rows, inputs, gain_one.astype(jnp.float32))
    normed_one = normed_one_f.astype(jnp.bfloat16)
    query_raw = jnp.dot(normed_one, query_full, preferred_element_type=jnp.float32)
    keyval_raw = jnp.dot(normed_one, keyval_full, preferred_element_type=jnp.float32)

    def turn_rows(v):
        return rotate(v, positions)

    query_rot, query_pull = jax.vjp(
        turn_rows, query_raw.reshape(row_count, HEADS, HD).transpose(1, 0, 2)
    )
    key_rot, key_pull = jax.vjp(turn_rows, keyval_raw[:, :HD])
    queries = query_rot.astype(jnp.bfloat16).reshape(HEADS * row_count, HD)
    keyval_own = jnp.concatenate([key_rot, keyval_raw[:, HD:]], axis=1).astype(jnp.bfloat16)

    def pass_forward(carried, unused):
        moved = shifted(carried, "seq", 1)
        return (moved, moved)

    _, earlier = lax.scan(pass_forward, keyval_own, None, length=depth)
    keyval_all = jnp.concatenate([keyval_own[None], earlier], axis=0).reshape(
        (depth + 1) * row_count, 2 * HD
    )
    key_rows = keyval_all[:, :HD]
    value_rows = keyval_all[:, HD:]
    offsets = jnp.arange(depth + 1, dtype=jnp.int32)
    key_pos = (
        (seq_place - offsets)[:, None] * row_count + jnp.arange(row_count, dtype=jnp.int32)[None, :]
    ).reshape(-1)
    query_pos = jnp.tile(positions, HEADS)
    distance = query_pos[:, None] - key_pos[None, :]
    allowed = (distance >= 0) & (distance < WINDOW) & (key_pos[None, :] >= 0)

    def score_block():
        raw_scores = contract_last(queries, key_rows) * score_scale
        return jnp.where(allowed, raw_scores, -1e30)

    scores = score_block()
    row_max = jnp.max(scores, axis=1, keepdims=True)
    exponent = jnp.exp(scores - row_max)
    row_total = jnp.sum(exponent, axis=1, keepdims=True)
    probs = exponent / row_total
    log_total = row_max + jnp.log(row_total)
    mixed_heads = jnp.dot(
        probs.astype(jnp.bfloat16), value_rows, preferred_element_type=jnp.float32
    )
    mixed_low = (
        mixed_heads.reshape(HEADS, row_count, HD)
        .transpose(1, 0, 2)
        .reshape(row_count, HEADS * HD)
        .astype(jnp.bfloat16)
    )
    resid = inputs + contract_last(mixed_low, out_full)
    normed_two_f, norm_two_pull = jax.vjp(norm_rows, resid, gain_two.astype(jnp.float32))
    normed_two = normed_two_f.astype(jnp.bfloat16)
    gate_pre = jnp.dot(normed_two, gate_full, preferred_element_type=jnp.float32)
    upward = jnp.dot(normed_two, up_full, preferred_element_type=jnp.float32)
    gelu_value, gelu_pull = jax.vjp(gelu_tanh, gate_pre)
    hidden = (gelu_value * upward).astype(jnp.bfloat16)
    output_rows = (resid + contract_last(hidden, down_full)).astype(jnp.bfloat16)
    back_part = (
        lax.all_gather(w_query, "seq", axis=1, tiled=True),
        lax.all_gather(w_keyval, "seq", axis=1, tiled=True),
        lax.all_gather(w_out, "seq", axis=1, tiled=True),
        lax.all_gather(w_gate, "seq", axis=1, tiled=True),
        lax.all_gather(w_up, "seq", axis=1, tiled=True),
        lax.all_gather(w_down, "seq", axis=1, tiled=True),
    )
    query_back, keyval_back, out_back, gate_back, up_back, down_back = (
        lax.all_gather(back_part[0], "dp", axis=0, tiled=True),
        lax.all_gather(back_part[1], "dp", axis=0, tiled=True),
        lax.all_gather(back_part[2], "dp", axis=0, tiled=True),
        lax.all_gather(back_part[3], "dp", axis=0, tiled=True),
        lax.all_gather(back_part[4], "dp", axis=0, tiled=True),
        lax.all_gather(back_part[5], "dp", axis=0, tiled=True),
    )
    upstream = cotangent.astype(jnp.float32)
    grad_hidden = jnp.dot(cotangent, down_back, preferred_element_type=jnp.float32)
    grad_gate = gelu_pull(grad_hidden * upward)[0].astype(jnp.bfloat16)
    grad_upward = (grad_hidden * gelu_value).astype(jnp.bfloat16)
    grad_normed_two = contract_last(grad_gate, gate_back) + contract_last(grad_upward, up_back)
    grad_resid_part, grad_gain_two = norm_two_pull(grad_normed_two)
    grad_resid = upstream + grad_resid_part
    normed_two_seq, cotangent_seq = (
        lax.all_gather(normed_two, "seq", axis=0, tiled=True),
        lax.all_gather(cotangent, "seq", axis=0, tiled=True),
    )
    gate_cols, upward_cols, hidden_cols = (
        lax.all_to_all(grad_gate, "seq", split_axis=1, concat_axis=0, tiled=True),
        lax.all_to_all(grad_upward, "seq", split_axis=1, concat_axis=0, tiled=True),
        lax.all_to_all(hidden, "seq", split_axis=1, concat_axis=0, tiled=True),
    )
    left_rows = normed_two_seq
    mlp_share = lax.psum_scatter(
        jnp.concatenate(
            [
                contract_rows(left_rows, gate_cols),
                contract_rows(left_rows, upward_cols),
                contract_rows(cotangent_seq, hidden_cols),
            ],
            axis=1,
        ).astype(jnp.bfloat16),
        "dp",
        scatter_dimension=0,
        tiled=True,
    ).astype(jnp.float32)
    attn_low = grad_resid.astype(jnp.bfloat16)
    grad_mixed = jnp.dot(attn_low, out_back, preferred_element_type=jnp.float32).astype(
        jnp.bfloat16
    )
    grad_heads = (
        grad_mixed.reshape(row_count, HEADS, HD).transpose(1, 0, 2).reshape(HEADS * row_count, HD)
    )
    probs_again = jnp.exp(score_block() - log_total)
    grad_probs = contract_last(grad_heads, value_rows)
    grad_scores = (
        probs_again * (grad_probs - jnp.sum(probs_again * grad_probs, axis=1, keepdims=True))
    ).astype(jnp.bfloat16)
    grad_queries = jnp.dot(grad_scores, key_rows, preferred_element_type=jnp.float32) * score_scale
    grad_keys_all = contract_rows(grad_scores, queries) * score_scale
    grad_values_all = contract_rows(probs_again.astype(jnp.bfloat16), grad_heads)
    grad_keyval_all = jnp.concatenate([grad_keys_all, grad_values_all], axis=1).reshape(
        depth + 1, row_count, 2 * HD
    )

    def pass_backward(carried, piece_grad):
        return (
            shifted((carried + piece_grad).astype(jnp.bfloat16), "seq", -1).astype(jnp.float32),
            None,
        )

    returned, _ = lax.scan(
        pass_backward, jnp.zeros((row_count, 2 * HD), jnp.float32), grad_keyval_all[1:][::-1]
    )
    grad_keyval = grad_keyval_all[0] + returned
    grad_keys_raw = key_pull(grad_keyval[:, :HD])[0]
    grad_keyval_raw = jnp.concatenate([grad_keys_raw, grad_keyval[:, HD:]], axis=1).astype(
        jnp.bfloat16
    )
    grad_query_raw = (
        query_pull(grad_queries.reshape(HEADS, row_count, HD))[0]
        .transpose(1, 0, 2)
        .reshape(row_count, HEADS * HD)
        .astype(jnp.bfloat16)
    )
    grad_normed_one = contract_last(grad_query_raw, query_back) + contract_last(
        grad_keyval_raw, keyval_back
    )
    grad_in_part, grad_gain_one = norm_one_pull(grad_normed_one)
    grad_input = grad_resid + grad_in_part
    normed_one_seq, attn_low_seq = (
        lax.all_gather(normed_one, "seq", axis=0, tiled=True),
        lax.all_gather(attn_low, "seq", axis=0, tiled=True),
    )
    query_cols, keyval_cols, mixed_cols = (
        lax.all_to_all(grad_query_raw, "seq", split_axis=1, concat_axis=0, tiled=True),
        lax.all_to_all(grad_keyval_raw, "seq", split_axis=1, concat_axis=0, tiled=True),
        lax.all_to_all(mixed_low, "seq", split_axis=1, concat_axis=0, tiled=True),
    )
    left_rows = normed_one_seq
    attn_share = lax.psum_scatter(
        jnp.concatenate(
            [
                contract_rows(left_rows, query_cols),
                contract_rows(left_rows, keyval_cols),
                contract_rows(attn_low_seq, mixed_cols),
            ],
            axis=1,
        ).astype(jnp.bfloat16),
        "dp",
        scatter_dimension=0,
        tiled=True,
    ).astype(jnp.float32)
    gain_shares = (
        lax.psum_scatter(grad_gain_one, ("dp", "seq"), scatter_dimension=0, tiled=True),
        lax.psum_scatter(grad_gain_two, ("dp", "seq"), scatter_dimension=0, tiled=True),
    )
    query_width = w_query.shape[1]
    keyval_width = w_keyval.shape[1]
    ff_width = w_gate.shape[1]
    grad_w_query = attn_share[:, :query_width]
    grad_w_keyval = attn_share[:, query_width : query_width + keyval_width]
    grad_w_out = attn_share[:, query_width + keyval_width :]
    return (
        output_rows,
        grad_input,
        grad_w_query,
        grad_w_keyval,
        grad_w_out,
        gain_shares[0],
        mlp_share[:, :ff_width],
        mlp_share[:, ff_width : 2 * ff_width],
        mlp_share[:, 2 * ff_width :],
        gain_shares[1],
    )


def solution(mesh):
    placed = (
        P(("dp", "seq"), None),
        P("dp", "seq"),
        P("dp", "seq"),
        P("dp", "seq"),
        P(("dp", "seq")),
        P("dp", "seq"),
        P("dp", "seq"),
        P("dp", "seq"),
        P(("dp", "seq")),
        P(("dp", "seq"), None),
    )
    return jax.shard_map(
        local,
        mesh=mesh,
        in_specs=placed,
        out_specs=(
            P(("dp", "seq"), None),
            P(("dp", "seq"), None),
            P("dp", "seq"),
            P("dp", "seq"),
            P("dp", "seq"),
            P(("dp", "seq")),
            P("dp", "seq"),
            P("dp", "seq"),
            P("dp", "seq"),
            P(("dp", "seq")),
        ),
        check_vma=False,
    )
```

profile of v0, /device:TPU:0, one launch (start us, length us, event | category | flops | bytes accessed | tf_op | source)
XLA Modules:
  0.0 3644.4 jit_solution(13936530598048494936)
XLA Ops:
  10.6 37.0 %all_gather.76 = bf16[640,512]{0,1:T(8,128)(2,1)} all-gather(bf16[640,64]{0,1:T(8,128)(2,1)} %param.16), channel_id=1, replica_groups=mesh['dp'=4,'seq'=8] {'seq'}, dimensions={1}, use_global_device_ids=true | all-gather | bytes 737280 | tf_op jit(solution)/shard_map/all_gather | solution.py:68
  47.6 30.3 all-gather.18.cloned.1.call-done
  78.0 62.6 %all-gather.24.cloned.1.call-done = bf16[640,2560]{0,1:T(8,128)(2,1)} async-done(((bf16[640,320]{0,1:T(8,128)(2,1)}), bf16[640,2560]{0,1:T(8,128)(2,1)}) %all-gather.24.cloned.1.call-update) | async-done | bytes 3276816 | tf_op jit(solution)/shard_map/all_gather | solution.py:69
  140.7 143.1 %all-gather.28.cloned.1.call-done = bf16[640,7680]{0,1:T(8,128)(2,1)} async-done(((bf16[640,960]{0,1:T(8,128)(2,1)}), bf16[640,7680]{0,1:T(8,128)(2,1)}) %all-gather.28.cloned.1.call-update) | async-done | bytes 9830416 | tf_op jit(solution)/shard_map/all_gather | solution.py:70
  283.8 142.4 %all-gather.32.cloned.1.call-done = bf16[640,7680]{0,1:T(8,128)(2,1)} async-done(((bf16[640,960]{0,1:T(8,128)(2,1)}), bf16[640,7680]{0,1:T(8,128)(2,1)}) %all-gather.32.cloned.1.call-update) | async-done | bytes 9830416 | tf_op jit(solution)/shard_map/all_gather | solution.py:71
  426.3 142.3 %all-gather.36.cloned.1.call-done = bf16[640,7680]{0,1:T(8,128)(2,1)} async-done(((bf16[640,960]{0,1:T(8,128)(2,1)}), bf16[640,7680]{0,1:T(8,128)(2,1)}) %all-gather.36.cloned.1.call-update) | async-done | bytes 9830416 | tf_op jit(solution)/shard_map/all_gather | solution.py:72
  610.0 61.6 %while.23 = (s32[]{:T(128)}, bf16[512,512]{1,0:T(8,128)(2,1)S(1)}, bf16[4,512,512]{2,1,0:T(8,128)(2,1)}, s32[]{:T(128)}) while((s32[]{:T(128)}, bf16[512,512]{1,0:T(8,128)(2,1)S(1)}, bf16[4,512,512]{2,1,0:T(8,128)(2,1)}, s32[]{:T(128)}) %tuple.62), condition=%wide.region_2.3_spmd, body=%wide.region_1.2_spmd.sunk | while | flops 2 | bytes 4194409 | solution.py:106
  704.0 29.9 fusion.58
  798.1 206.0 %all-gather.30.cloned.1.call-done = bf16[2560,7680]{0,1:T(8,128)(2,1)} async-done(((bf16[640,7680]{0,1:T(8,128)(2,1)}), bf16[2560,7680]{0,1:T(8,128)(2,1)}) %all-gather.30.cloned.1.call-update) | async-done | bytes 39321616 | tf_op jit(solution)/shard_map/all_gather | solution.py:80
  1004.1 32.0 fusion.61
  1036.1 204.9 %all-gather.34.cloned.1.call-done = bf16[2560,7680]{0,1:T(8,128)(2,1)} async-done(((bf16[640,7680]{0,1:T(8,128)(2,1)}), bf16[2560,7680]{0,1:T(8,128)(2,1)}) %all-gather.34.cloned.1.call-update) | async-done | bytes 39321616 | tf_op jit(solution)/shard_map/all_gather | solution.py:81
  1241.1 32.3 fusion.62
  1273.4 204.8 %all-gather.38.cloned.1.call-done = bf16[2560,7680]{0,1:T(8,128)(2,1)} async-done(((bf16[640,7680]{0,1:T(8,128)(2,1)}), bf16[2560,7680]{0,1:T(8,128)(2,1)}) %all-gather.38.cloned.1.call-update) | async-done | bytes 39321616 | tf_op jit(solution)/shard_map/all_gather | solution.py:82
  1478.2 39.7 %multiply_convert_fusion.1 = (bf16[512,7680]{1,0:T(8,128)(2,1)}, bf16[512,7680]{1,0:T(8,128)(2,1)}, bf16[512,7680]{1,0:T(8,128)(2,1)}) fusion(f32[512,7680]{1,0:T(8,128)} %fusion.61, f32[512,7680]{1,0:T(8,128)} %fusion.62, bf16[512,2560]{1,0:T(8,128)(2,1)S(1)} %copy-done.4, bf16[2560,7680]{0,1:T(8,128)(2,1)} %all-gather.38.cloned.1.call-done), kind=kOutput, calls=%fused_computation.27 | convolution fusion | flops 20234895360 | bytes 96993280 | tf_op jit(solution)/shard_map/dot_general | solution.py:164
  1573.6 196.7 %all-to-all-done.5 = bf16[512,8,960]{0,2,1:T(8,128)(2,1)} async-done(((bf16[512,8,960]{0,2,1:T(8,128)(2,1)}), bf16[512,8,960]{0,2,1:T(8,128)(2,1)}, u32[]{:S(2)}, u32[]{:S(2)}) %all-to-all-start.5) | async-done | bytes 7864352 | tf_op jit(solution)/shard_map/all_to_all | solution.py:177
  1770.3 60.0 %all-to-all-start.4 = ((bf16[512,8,960]{0,2,1:T(8,128)(2,1)}), bf16[512,8,960]{0,2,1:T(8,128)(2,1)}, u32[]{:S(2)}, u32[]{:S(2)}) async-start(bf16[512,8,960]{0,2,1:T(8,128)(2,1)} %bitcast.107), calls=%async_computation.4 | async-start | bytes 15728640 | tf_op jit(solution)/shard_map/all_to_all | solution.py:176
  1878.5 180.1 %all-to-all-done.4 = bf16[512,8,960]{0,2,1:T(8,128)(2,1)} async-done(((bf16[512,8,960]{0,2,1:T(8,128)(2,1)}), bf16[512,8,960]{0,2,1:T(8,128)(2,1)}, u32[]{:S(2)}, u32[]{:S(2)}) %all-to-all-start.4) | async-done | bytes 7864352 | tf_op jit(solution)/shard_map/all_to_all | solution.py:176
  2058.7 44.9 %all-to-all-start.3 = ((bf16[512,8,960]{0,2,1:T(8,128)(2,1)}), bf16[512,8,960]{0,2,1:T(8,128)(2,1)}, u32[]{:S(2)}, u32[]{:S(2)}) async-start(bf16[512,8,960]{0,2,1:T(8,128)(2,1)} %bitcast.108), calls=%async_computation.3 | async-start | bytes 15728640 | tf_op jit(solution)/shard_map/all_to_all | solution.py:175
  2137.3 202.1 %all-to-all-done.3 = bf16[512,8,960]{0,2,1:T(8,128)(2,1)} async-done(((bf16[512,8,960]{0,2,1:T(8,128)(2,1)}), bf16[512,8,960]{0,2,1:T(8,128)(2,1)}, u32[]{:S(2)}, u32[]{:S(2)}) %all-to-all-start.3) | async-done | bytes 7864352 | tf_op jit(solution)/shard_map/all_to_all | solution.py:175
  2339.4 57.7 %all-to-all-start.2 = ((bf16[512,8,320]{0,2,1:T(8,128)(2,1)}), bf16[512,8,320]{0,2,1:T(8,128)(2,1)}, u32[]{:S(2)}, u32[]{:S(2)}) async-start(bf16[512,8,320]{0,2,1:T(8,128)(2,1)} %bitcast.116), calls=%async_computation.2 | async-start | bytes 5242880 | tf_op jit(solution)/shard_map/all_to_all | solution.py:244
  2453.6 123.2 %all-gather.46.cloned.1.call-done = bf16[4096,2560]{1,0:T(8,128)(2,1)} async-done(((bf16[512,2560]{1,0:T(8,128)(2,1)}), bf16[4096,2560]{1,0:T(8,128)(2,1)}) %all-gather.46.cloned.1.call-update) | async-done | bytes 20971536 | tf_op jit(solution)/shard_map/all_gather | solution.py:172
  2665.0 33.6 multiply_reduce_fusion
  2698.6 41.6 %multiply_convert_fusion = bf16[5120,2560]{0,1:T(8,128)(2,1)} fusion(f32[5120,2560]{0,1:T(8,128)} %get-tuple-element.115, f32[5120,2560]{0,1:T(8,128)} %get-tuple-element.110, f32[5120]{0:T(1024)S(1)} %get-tuple-element.114, f32[5120]{0:T(1024)S(1)} %log_add_fusion), kind=kLoop, calls=%fused_computation.5 | loop fusion | flops 52428800 | bytes 131112960 | tf_op jit(solution)/shard_map/convert_element_type | solution.py:204
  2769.5 195.0 %while.24 = (s32[]{:T(128)}, f32[512,512]{1,0:T(8,128)S(1)}, f32[4,512,512]{2,1,0:T(8,128)}, s32[]{:T(128)}, s32[]{:T(128)}) while((s32[]{:T(128)}, f32[512,512]{1,0:T(8,128)S(1)}, f32[4,512,512]{2,1,0:T(8,128)}, s32[]{:T(128)}, s32[]{:T(128)}) %tuple.102), condition=%wide.region_9.10_spmd.clone, body=%wide.region_8.9_spmd.clone.sunk | while | flops 1048579 | bytes 6291571 | solution.py:218
  2772.3 70.2 %collective-permute-done.1 = bf16[512,512]{1,0:T(8,128)(2,1)S(1)} collective-permute-done((bf16[512,512]{1,0:T(8,128)(2,1)S(1)}, bf16[512,512]{1,0:T(8,128)(2,1)S(1)}, u32[]{:S(2)}, u32[]{:S(2)}) %collective-permute-start.1) | collective-permute-done | bytes 524320 | tf_op jit(solution)/shard_map/while/body/eval_jaxpr/ppermute | solution.py:14
  2845.5 40.5 %collective-permute-done.1 = bf16[512,512]{1,0:T(8,128)(2,1)S(1)} collective-permute-done((bf16[512,512]{1,0:T(8,128)(2,1)S(1)}, bf16[512,512]{1,0:T(8,128)(2,1)S(1)}, u32[]{:S(2)}, u32[]{:S(2)}) %collective-permute-start.1) | collective-permute-done | bytes 524320 | tf_op jit(solution)/shard_map/while/body/eval_jaxpr/ppermute | solution.py:14
  2888.9 34.0 collective-permute-done.1
  2925.8 38.5 %collective-permute-done.1 = bf16[512,512]{1,0:T(8,128)(2,1)S(1)} collective-permute-done((bf16[512,512]{1,0:T(8,128)(2,1)S(1)}, bf16[512,512]{1,0:T(8,128)(2,1)S(1)}, u32[]{:S(2)}, u32[]{:S(2)}) %collective-permute-start.1) | collective-permute-done | bytes 524320 | tf_op jit(solution)/shard_map/while/body/eval_jaxpr/ppermute | solution.py:14
  3068.4 30.6 all-to-all-done
  3112.0 352.8 %all-gather.42.cloned.1.call-done = bf16[4096,2560]{1,0:T(8,128)(2,1)} async-done(((bf16[512,2560]{1,0:T(8,128)(2,1)}), bf16[4096,2560]{1,0:T(8,128)(2,1)}) %all-gather.42.cloned.1.call-update) | async-done | bytes 20971536 | tf_op jit(solution)/shard_map/all_gather | solution.py:239
  3494.2 44.3 %all-reduce.10 = (f32[2560]{0:T(1024)S(1)}, f32[2560]{0:T(1024)S(1)}) all-reduce(f32[2560]{0:T(1024)S(1)} %get-tuple-element.69, f32[2560]{0:T(1024)S(1)} %copy-done.51), channel_id=3, replica_groups=mesh['dp'=4,'seq'=8] {'dp','seq'}, use_global_device_ids=true, to_apply=%region_13.14.clone | all-reduce | flops 5120 | bytes 40960
  3600.8 32.9 reduce-scatter.7.cloned.1.call-done
  (306 shorter events, 737.1 us)
Async XLA Ops:
  7.2 70.7 %all-gather.18.cloned.1.call-start = ((), (), s32[]{:S(2)}) async-start(), calls=%async_computation.8 | async-start | bytes 3686400 | tf_op jit(solution)/shard_map/all_gather | solution.py:67
  7.9 132.7 %all-gather.24.cloned.1.call-start = ((), (), s32[]{:S(2)}) async-start(), calls=%async_computation.11 | async-start | bytes 3686400 | tf_op jit(solution)/shard_map/all_gather | solution.py:69
  8.7 275.1 %all-gather.28.cloned.1.call-start = ((), (), s32[]{:S(2)}) async-start(), calls=%async_computation.13 | async-start | bytes 11059200 | tf_op jit(solution)/shard_map/all_gather | solution.py:70
  9.4 416.8 %all-gather.32.cloned.1.call-start = ((), (), s32[]{:S(2)}) async-start(), calls=%async_computation.15 | async-start | bytes 11059200 | tf_op jit(solution)/shard_map/all_gather | solution.py:71
  10.0 558.7 %all-gather.36.cloned.1.call-start = ((), (), s32[]{:S(2)}) async-start(), calls=%async_computation.17 | async-start | bytes 11059200 | tf_op jit(solution)/shard_map/all_gather | solution.py:72
  10.6 593.0 %all-gather.22.cloned.1.call-start = ((), (), s32[]{:S(2)}) async-start(), calls=%async_computation.10 | async-start | bytes 3276800 | tf_op jit(solution)/shard_map/all_gather | solution.py:78
  47.6 632.8 %all-gather.20.cloned.1.call-start = ((), (), s32[]{:S(2)}) async-start(), calls=%async_computation.9 | async-start | bytes 16384000 | tf_op jit(solution)/shard_map/all_gather | solution.py:77
  77.9 698.8 %all-gather.26.cloned.1.call-start = ((), (), s32[]{:S(2)}) async-start(), calls=%async_computation.12 | async-start | bytes 16384000 | tf_op jit(solution)/shard_map/all_gather | solution.py:79
  140.6 863.5 %all-gather.30.cloned.1.call-start = ((), (), s32[]{:S(2)}) async-start(), calls=%async_computation.14 | async-start | bytes 49152000 | tf_op jit(solution)/shard_map/all_gather | solution.py:80
  283.7 957.3 %all-gather.34.cloned.1.call-start = ((), (), s32[]{:S(2)}) async-start(), calls=%async_computation.16 | async-start | bytes 49152000 | tf_op jit(solution)/shard_map/all_gather | solution.py:81
  426.3 1051.9 %all-gather.38.cloned.1.call-start = ((), (), s32[]{:S(2)}) async-start(), calls=%async_computation.18 | async-start | bytes 49152000 | tf_op jit(solution)/shard_map/all_gather | solution.py:82
  568.7 1836.0 %all-gather.44.cloned.1.call-start = ((), (), s32[]{:S(2)}) async-start(), calls=%async_computation.21 | async-start | bytes 23592960 | tf_op jit(solution)/shard_map/all_gather | solution.py:171
  610.2 14.1 collective-permute-start
  625.2 15.4 collective-permute-start
  641.5 14.6 collective-permute-start
  656.9 13.9 collective-permute-start
  796.7 1780.0 %all-gather.46.cloned.1.call-start = ((), (), s32[]{:S(2)}) async-start(), calls=%async_computation.22 | async-start | bytes 23592960 | tf_op jit(solution)/shard_map/all_gather | solution.py:172
  797.5 2261.8 %all-gather.40.cloned.1.call-start = ((), (), s32[]{:S(2)}) async-start(), calls=%async_computation.19 | async-start | bytes 23592960 | tf_op jit(solution)/shard_map/all_gather | solution.py:238
  1036.1 442.1 %copy-start.4 = (bf16[512,2560]{1,0:T(8,128)(2,1)S(1)}, bf16[512,2560]{1,0:T(8,128)(2,1)}, u32[]{:S(2)}) copy-start(bf16[512,2560]{1,0:T(8,128)(2,1)} %param.23) | copy-start | bytes 7864324
  1528.5 241.8 %all-to-all-start.5 = ((bf16[512,8,960]{0,2,1:T(8,128)(2,1)}), bf16[512,8,960]{0,2,1:T(8,128)(2,1)}, u32[]{:S(2)}, u32[]{:S(2)}) async-start(bf16[512,8,960]{0,2,1:T(8,128)(2,1)} %bitcast.109), calls=%async_computation.5 | async-start | bytes 15728640 | tf_op jit(solution)/shard_map/all_to_all | solution.py:177
  1770.3 288.3 %all-to-all-start.4 = ((bf16[512,8,960]{0,2,1:T(8,128)(2,1)}), bf16[512,8,960]{0,2,1:T(8,128)(2,1)}, u32[]{:S(2)}, u32[]{:S(2)}) async-start(bf16[512,8,960]{0,2,1:T(8,128)(2,1)} %bitcast.107), calls=%async_computation.4 | async-start | bytes 15728640 | tf_op jit(solution)/shard_map/all_to_all | solution.py:176
  1830.4 1634.4 %all-gather.42.cloned.1.call-start = ((), (), s32[]{:S(2)}) async-start(), calls=%async_computation.20 | async-start | bytes 23592960 | tf_op jit(solution)/shard_map/all_gather | solution.py:239
  2058.7 280.7 %all-to-all-start.3 = ((bf16[512,8,960]{0,2,1:T(8,128)(2,1)}), bf16[512,8,960]{0,2,1:T(8,128)(2,1)}, u32[]{:S(2)}, u32[]{:S(2)}) async-start(bf16[512,8,960]{0,2,1:T(8,128)(2,1)} %bitcast.108), calls=%async_computation.3 | async-start | bytes 15728640 | tf_op jit(solution)/shard_map/all_to_all | solution.py:175
  2339.4 644.9 %all-to-all-start.2 = ((bf16[512,8,320]{0,2,1:T(8,128)(2,1)}), bf16[512,8,320]{0,2,1:T(8,128)(2,1)}, u32[]{:S(2)}, u32[]{:S(2)}) async-start(bf16[512,8,320]{0,2,1:T(8,128)(2,1)} %bitcast.116), calls=%async_computation.2 | async-start | bytes 5242880 | tf_op jit(solution)/shard_map/all_to_all | solution.py:244
  2397.1 1191.5 %reduce-scatter.9.cloned.1.call-start = ((), (), s32[]{:S(2)}) async-start(), calls=%async_computation.24 | async-start | bytes 18841600
  2771.0 71.5 %collective-permute-start.1 = (bf16[512,512]{1,0:T(8,128)(2,1)S(1)}, bf16[512,512]{1,0:T(8,128)(2,1)S(1)}, u32[]{:S(2)}, u32[]{:S(2)}) collective-permute-start(bf16[512,512]{1,0:T(8,128)(2,1)S(1)} %fusion.105), channel_id=1, source_target_pairs={{1,0},{2,1},{3,2},{4,3},{5,4},{6,5},{7,6},{9,8},{10,9},{11,10},{12... | collective-permute-start | bytes 1572872 | tf_op jit(solution)/shard_map/while/body/eval_jaxpr/ppermute | solution.py:14
  2844.2 41.8 %collective-permute-start.1 = (bf16[512,512]{1,0:T(8,128)(2,1)S(1)}, bf16[512,512]{1,0:T(8,128)(2,1)S(1)}, u32[]{:S(2)}, u32[]{:S(2)}) collective-permute-start(bf16[512,512]{1,0:T(8,128)(2,1)S(1)} %fusion.105), channel_id=1, source_target_pairs={{1,0},{2,1},{3,2},{4,3},{5,4},{6,5},{7,6},{9,8},{10,9},{11,10},{12... | collective-permute-start | bytes 1572872 | tf_op jit(solution)/shard_map/while/body/eval_jaxpr/ppermute | solution.py:14
  2887.6 35.3 collective-permute-start.1
  2924.5 39.8 %collective-permute-start.1 = (bf16[512,512]{1,0:T(8,128)(2,1)S(1)}, bf16[512,512]{1,0:T(8,128)(2,1)S(1)}, u32[]{:S(2)}, u32[]{:S(2)}) collective-permute-start(bf16[512,512]{1,0:T(8,128)(2,1)S(1)} %fusion.105), channel_id=1, source_target_pairs={{1,0},{2,1},{3,2},{4,3},{5,4},{6,5},{7,6},{9,8},{10,9},{11,10},{12... | collective-permute-start | bytes 1572872 | tf_op jit(solution)/shard_map/while/body/eval_jaxpr/ppermute | solution.py:14
  2984.3 21.7 all-to-all-start.1
  3006.0 93.0 %all-to-all-start = ((bf16[512,8,320]{0,2,1:T(8,128)(2,1)}), bf16[512,8,320]{0,2,1:T(8,128)(2,1)S(1)}, u32[]{:S(2)}, u32[]{:S(2)}) async-start(bf16[512,8,320]{0,2,1:T(8,128)(2,1)} %bitcast.119), calls=%async_computation | async-start | bytes 5242880 | tf_op jit(solution)/shard_map/all_to_all | solution.py:242
  3025.2 608.5 %reduce-scatter.7.cloned.1.call-start = ((), (), s32[]{:S(2)}) async-start(), calls=%async_computation.23 | async-start | bytes 4915200
  (61 other events, 2327.7 us)
Sparse Core Ops, SparseCore 0:
  10.2 67.6 all-gather.17
  80.1 60.4 all-gather.23
  142.8 140.8 all-gather.27
  285.8 140.3 all-gather.31
  428.2 140.3 all-gather.35
  570.1 23.6 all-gather.21
  595.4 84.9 all-gather.19
  682.0 84.9 all-gather.25
  768.5 235.5 all-gather.29
  1005.5 235.5 all-gather.33
  1242.6 235.5 all-gather.37
  1479.6 570.2 all-gather.43
  2051.4 525.3 all-gather.45
  2578.7 480.5 all-gather.39
  3060.7 404.0 all-gather.41
  3467.2 121.2 reduce-scatter.8
  3591.0 42.7 reduce-scatter.6
where the time goes:
time: 3650 us; the launch traced here: 3640 us
  waiting for transfers between devices  2520 us (69%)
  matrix products  491 us (13%)
  starting transfers between devices  213 us (6%)
  local copies, waits for them, and re-layouts  166 us (5%)
  other arithmetic  130 us (4%)
  blocking collectives  110 us (3%)
    all_gather x1, waiting for transfers between devices, local(): lax.all_gather(attn_low, 'seq', axis=0, tiled=True)  353 us
    ppermute x8, waiting for transfers between devices, shifted(): return lax.ppermute(shard, axis, pairs)  225 us
    all_gather x1, waiting for transfers between devices, local(): lax.all_gather(column_part[3], 'dp', axis=0, tiled=True)  206 us
    all_gather x1, waiting for transfers between devices, local(): lax.all_gather(column_part[4], 'dp', axis=0, tiled=True)  205 us
    all_gather x1, waiting for transfers between devices, local(): lax.all_gather(column_part[5], 'dp', axis=0, tiled=True)  205 us
    all_to_all x1, waiting for transfers between devices, local(): lax.all_to_all(grad_gate, 'seq', split_axis=1, concat_axis=0, tiled=True)  202 us
    all_to_all x1, waiting for transfers between devices, local(): lax.all_to_all(hidden, 'seq', split_axis=1, concat_axis=0, tiled=True)  197 us
    dot_general x8, matrix products, contract_last(): lax.dot_general(left, right, (((1,), (1,)), ((), ())), preferred_element_...  185 us
  transfers between devices with their start and end apart: 31, of which 26 were waited for; matrix products, arithmetic and copies ran while one was open for 21% of the time, Pallas kernels for 0%

commit v1 on v0

--- a/solution.py
+++ b/solution.py
@@ -6,6 +6,40 @@
 HEADS = 10
 HD = 256
 WINDOW = 2048
+
+
+def create_face_in(my_data, row_dim):
+    my_data = jnp.moveaxis(my_data, 0, row_dim)
+    wide_out = my_data.shape
+    return my_data.reshape(
+        *wide_out[:row_dim], wide_out[row_dim] * wide_out[row_dim + 1], *wide_out[row_dim + 2 :]
+    )
+
+
+def clear_rings(dim_no, group_axis, mine_x):
+    parts_n = lax.psum(1, group_axis)
+    parts_seen = []
+    for tick in tuple(range(parts_n)):
+        parts_seen.append((tick, (tick + 1) % parts_n))
+    crops = []
+    for p, t in parts_seen:
+        crops.append((t, p))
+    val2, x_new = ([], [])
+    for s in [*range(parts_n - 1)]:
+        if s % 2 == 0:
+            outer = lax.ppermute(
+                val2[-1] if val2 else mine_x, axis_name=group_axis, perm=parts_seen
+            )
+            val2.append(outer)
+        else:
+            x_new.append(
+                lax.ppermute(x_new[-1] if x_new else mine_x, axis_name=group_axis, perm=crops)
+            )
+    e_now = jnp.stack([*val2[::-1], mine_x, *x_new], axis=0)
+    before = lax.axis_index(group_axis)
+    v_now = before - len(val2)
+    e_now = e_now[(jnp.arange(parts_n) - v_now) % parts_n]
+    return create_face_in(e_now, dim_no)
 
 
 def shifted(shard, axis, by):
@@ -77,7 +111,7 @@
         lax.all_gather(column_part[0], "dp", axis=0, tiled=True),
         lax.all_gather(column_part[1], "dp", axis=0, tiled=True),
         lax.all_gather(column_part[2], "dp", axis=0, tiled=True),
-        lax.all_gather(column_part[3], "dp", axis=0, tiled=True),
+        clear_rings(0, "dp", column_part[3]),
         lax.all_gather(column_part[4], "dp", axis=0, tiled=True),
         lax.all_gather(column_part[5], "dp", axis=0, tiled=True),
         lax.all_gather(column_part[6], "dp", axis=0, tiled=True),

time: 3650 us -> 3960 us (1.085)
  waiting for transfers between devices: 2520 us -> 2700 us
  local copies, waits for them, and re-layouts: 166 us -> 280 us
    ppermute x0 -> x3, waiting for transfers between devices: none -> 716 us  [the longest x2 716 us: clear_rings(): lax.ppermute(val2[-1] if val2 else mine_x, axis_name=group_axis, perm=par...]
    all_gather x1, waiting for transfers between devices: 206 us -> 0.01 us  [local(): lax.all_gather(back_part[3], 'dp', axis=0, tiled=True)]
    all_gather x1, waiting for transfers between devices: 205 us -> 0.01 us  [local(): lax.all_gather(column_part[4], 'dp', axis=0, tiled=True)]
    all_gather x1, waiting for transfers between devices: 205 us -> 0.01 us  [local(): lax.all_gather(column_part[5], 'dp', axis=0, tiled=True)]
    all_gather x1, waiting for transfers between devices: 123 us -> 193 us  [local(): lax.all_gather(cotangent, 'seq', axis=0, tiled=True)]
    gather x0 -> x6, local copies, waits for them, and re-layouts: none -> 67.8 us  [clear_rings(): e_now = e_now[(jnp.arange(parts_n) - v_now) % parts_n]]
    unnamed x140 -> x149, local copies, waits for them, and re-layouts: 57.5 us -> 89.9 us
  transfers between devices with their start and end apart: 31 -> 34, of which waited for: 26 -> 25; matrix products, arithmetic and copies ran while one was open for 21% -> 23% of each run, Pallas kernels for 0% -> 0%
where the time goes in v1:
time: 3960 us; the launch traced here: 3950 us
  waiting for transfers between devices  2700 us (68%)
  matrix products  484 us (12%)
  local copies, waits for them, and re-layouts  280 us (7%)
  starting transfers between devices  197 us (5%)
  other arithmetic  162 us (4%)
  blocking collectives  108 us (3%)
    ppermute x2, waiting for transfers between devices, clear_rings(): lax.ppermute(val2[-1] if val2 else mine_x, axis_name=group_axis, perm=par...  716 us
    all_gather x1, waiting for transfers between devices, local(): lax.all_gather(attn_low, 'seq', axis=0, tiled=True)  359 us
    ppermute x8, waiting for transfers between devices, shifted(): return lax.ppermute(shard, axis, pairs)  228 us
    all_to_all x1, waiting for transfers between devices, local(): lax.all_to_all(hidden, 'seq', split_axis=1, concat_axis=0, tiled=True)  216 us
    all_gather x1, waiting for transfers between devices, local(): lax.all_gather(cotangent, 'seq', axis=0, tiled=True)  193 us
    all_to_all x1, waiting for transfers between devices, local(): lax.all_to_all(grad_upward, 'seq', split_axis=1, concat_axis=0, tiled=True)  190 us
    dot_general x8, matrix products, contract_last(): lax.dot_general(left, right, (((1,), (1,)), ((), ())), preferred_element_...  184 us
    all_to_all x1, waiting for transfers between devices, local(): lax.all_to_all(grad_gate, 'seq', split_axis=1, concat_axis=0, tiled=True)  180 us
  transfers between devices with their start and end apart: 34, of which 25 were waited for; matrix products, arithmetic and copies ran while one was open for 23% of the time, Pallas kernels for 0%

profile of v1, /device:TPU:0, one launch (start us, length us, event | category | flops | bytes accessed | tf_op | source)
XLA Modules:
  0.0 3949.7 jit_solution(17756213686028022970)
XLA Ops:
  10.6 37.0 all_gather.75
  47.6 30.3 all-gather.18.cloned.1.call-done
  78.0 62.6 %all-gather.24.cloned.1.call-done = bf16[640,2560]{0,1:T(8,128)(2,1)} async-done(((bf16[640,320]{0,1:T(8,128)(2,1)}), bf16[640,2560]{0,1:T(8,128)(2,1)}) %all-gather.24.cloned.1.call-update) | async-done | bytes 3276816 | tf_op jit(solution)/shard_map/all_gather | solution.py:103
  140.7 143.1 %all-gather.30.cloned.1.call-done = bf16[640,7680]{0,1:T(8,128)(2,1)} async-done(((bf16[640,960]{0,1:T(8,128)(2,1)}), bf16[640,7680]{0,1:T(8,128)(2,1)}) %all-gather.30.cloned.1.call-update) | async-done | bytes 9830416 | tf_op jit(solution)/shard_map/all_gather | solution.py:105
  283.8 142.4 %all-gather.34.cloned.1.call-done = bf16[640,7680]{0,1:T(8,128)(2,1)} async-done(((bf16[640,960]{0,1:T(8,128)(2,1)}), bf16[640,7680]{0,1:T(8,128)(2,1)}) %all-gather.34.cloned.1.call-update) | async-done | bytes 9830416 | tf_op jit(solution)/shard_map/all_gather | solution.py:106
  426.3 142.3 %all-gather.28.cloned.1.call-done = bf16[640,7680]{0,1:T(8,128)(2,1)} async-done(((bf16[640,960]{0,1:T(8,128)(2,1)}), bf16[640,7680]{0,1:T(8,128)(2,1)}) %all-gather.28.cloned.1.call-update) | async-done | bytes 9830416 | tf_op jit(solution)/shard_map/all_gather | solution.py:104
  610.0 61.7 %while.23 = (s32[]{:T(128)}, bf16[512,512]{1,0:T(8,128)(2,1)S(1)}, bf16[4,512,512]{2,1,0:T(8,128)(2,1)}, s32[]{:T(128)}) while((s32[]{:T(128)}, bf16[512,512]{1,0:T(8,128)(2,1)S(1)}, bf16[4,512,512]{2,1,0:T(8,128)(2,1)}, s32[]{:T(128)}) %tuple.67), condition=%wide.region_2.3_spmd, body=%wide.region_1.2_spmd.sunk | while | flops 2 | bytes 4194409 | solution.py:140
  704.0 29.8 fusion.61
  813.3 398.4 %collective-permute-done.2 = bf16[640,7680]{1,0:T(8,128)(2,1)} collective-permute-done((bf16[640,7680]{1,0:T(8,128)(2,1)}, bf16[640,7680]{1,0:T(8,128)(2,1)}, u32[]{:S(2)}, u32[]{:S(2)}) %collective-permute-start.2) | collective-permute-done | bytes 9830432 | tf_op jit(solution)/shard_map/ppermute | solution.py:30
  1211.8 318.0 %collective-permute-done.3 = bf16[640,7680]{1,0:T(8,128)(2,1)} collective-permute-done((bf16[640,7680]{1,0:T(8,128)(2,1)}, bf16[640,7680]{1,0:T(8,128)(2,1)}, u32[]{:S(2)}, u32[]{:S(2)}) %collective-permute-start.3) | collective-permute-done | bytes 9830432 | tf_op jit(solution)/shard_map/ppermute | solution.py:30
  1529.8 31.6 pad_maximum_fusion
  1689.2 29.2 fusion.65
  1718.4 40.0 %multiply_convert_fusion.1 = (bf16[512,7680]{1,0:T(8,128)(2,1)}, bf16[512,7680]{1,0:T(8,128)(2,1)}, bf16[512,7680]{1,0:T(8,128)(2,1)}) fusion(f32[512,7680]{1,0:T(8,128)} %fusion.64, f32[512,7680]{1,0:T(8,128)} %fusion.65, bf16[512,2560]{1,0:T(8,128)(2,1)S(1)} %copy-done.4, bf16[2560,7680]{0,1:T(8,128)(2,1)} %all-gather.36.cloned.1.call-done), kind=kOutput, calls=%fused_computation.33 | convolution fusion | flops 20234895360 | bytes 96993280 | tf_op jit(solution)/shard_map/dot_general | solution.py:198
  1814.7 215.7 %all-to-all-done.5 = bf16[512,8,960]{0,2,1:T(8,128)(2,1)} async-done(((bf16[512,8,960]{0,2,1:T(8,128)(2,1)}), bf16[512,8,960]{0,2,1:T(8,128)(2,1)}, u32[]{:S(2)}, u32[]{:S(2)}) %all-to-all-start.5) | async-done | bytes 7864352 | tf_op jit(solution)/shard_map/all_to_all | solution.py:211
  2030.4 46.3 %all-to-all-start.4 = ((bf16[512,8,960]{0,2,1:T(8,128)(2,1)}), bf16[512,8,960]{0,2,1:T(8,128)(2,1)}, u32[]{:S(2)}, u32[]{:S(2)}) async-start(bf16[512,8,960]{0,2,1:T(8,128)(2,1)} %bitcast.117), calls=%async_computation.4 | async-start | bytes 15728640 | tf_op jit(solution)/shard_map/all_to_all | solution.py:210
  2076.8 29.2 multiply_reduce_fusion.1
  2124.9 189.7 %all-to-all-done.4 = bf16[512,8,960]{0,2,1:T(8,128)(2,1)} async-done(((bf16[512,8,960]{0,2,1:T(8,128)(2,1)}), bf16[512,8,960]{0,2,1:T(8,128)(2,1)}, u32[]{:S(2)}, u32[]{:S(2)}) %all-to-all-start.4) | async-done | bytes 7864352 | tf_op jit(solution)/shard_map/all_to_all | solution.py:210
  2314.7 31.8 all-to-all-start.3
  2380.2 180.2 %all-to-all-done.3 = bf16[512,8,960]{0,2,1:T(8,128)(2,1)} async-done(((bf16[512,8,960]{0,2,1:T(8,128)(2,1)}), bf16[512,8,960]{0,2,1:T(8,128)(2,1)}, u32[]{:S(2)}, u32[]{:S(2)}) %all-to-all-start.3) | async-done | bytes 7864352 | tf_op jit(solution)/shard_map/all_to_all | solution.py:209
  2560.4 67.3 %all-to-all-start.2 = ((bf16[512,8,320]{0,2,1:T(8,128)(2,1)}), bf16[512,8,320]{0,2,1:T(8,128)(2,1)}, u32[]{:S(2)}, u32[]{:S(2)}) async-start(bf16[512,8,320]{0,2,1:T(8,128)(2,1)} %bitcast.126), calls=%async_computation.2 | async-start | bytes 5242880 | tf_op jit(solution)/shard_map/all_to_all | solution.py:278
  2684.3 192.8 %all-gather.46.cloned.1.call-done = bf16[4096,2560]{1,0:T(8,128)(2,1)} async-done(((bf16[512,2560]{1,0:T(8,128)(2,1)}), bf16[4096,2560]{1,0:T(8,128)(2,1)}) %all-gather.46.cloned.1.call-update) | async-done | bytes 20971536 | tf_op jit(solution)/shard_map/all_gather | solution.py:206
  2965.2 34.0 multiply_reduce_fusion
  2999.2 41.7 %multiply_convert_fusion = bf16[5120,2560]{0,1:T(8,128)(2,1)} fusion(f32[5120,2560]{0,1:T(8,128)} %get-tuple-element.123, f32[5120,2560]{0,1:T(8,128)} %get-tuple-element.118, f32[5120]{0:T(1024)S(1)} %get-tuple-element.122, f32[5120]{0:T(1024)S(1)} %log_add_fusion), kind=kLoop, calls=%fused_computation.10 | loop fusion | flops 52428800 | bytes 131112960 | tf_op jit(solution)/shard_map/convert_element_type | solution.py:238
  3070.2 197.3 %while.24 = (s32[]{:T(128)}, f32[512,512]{1,0:T(8,128)S(1)}, f32[4,512,512]{2,1,0:T(8,128)}, s32[]{:T(128)}, s32[]{:T(128)}) while((s32[]{:T(128)}, f32[512,512]{1,0:T(8,128)S(1)}, f32[4,512,512]{2,1,0:T(8,128)}, s32[]{:T(128)}, s32[]{:T(128)}) %tuple.107), condition=%wide.region_9.10_spmd.clone, body=%wide.region_8.9_spmd.clone.sunk | while | flops 1048579 | bytes 6291571 | solution.py:252
  3073.0 72.4 %collective-permute-done.1 = bf16[512,512]{1,0:T(8,128)(2,1)S(1)} collective-permute-done((bf16[512,512]{1,0:T(8,128)(2,1)S(1)}, bf16[512,512]{1,0:T(8,128)(2,1)S(1)}, u32[]{:S(2)}, u32[]{:S(2)}) %collective-permute-start.1) | collective-permute-done | bytes 524320 | tf_op jit(solution)/shard_map/while/body/eval_jaxpr/ppermute | solution.py:48
  3148.4 40.5 %collective-permute-done.1 = bf16[512,512]{1,0:T(8,128)(2,1)S(1)} collective-permute-done((bf16[512,512]{1,0:T(8,128)(2,1)S(1)}, bf16[512,512]{1,0:T(8,128)(2,1)S(1)}, u32[]{:S(2)}, u32[]{:S(2)}) %collective-permute-start.1) | collective-permute-done | bytes 524320 | tf_op jit(solution)/shard_map/while/body/eval_jaxpr/ppermute | solution.py:48
  3191.8 34.0 collective-permute-done.1
  3228.8 38.5 collective-permute-done.1
  3366.3 34.3 all-to-all-done
  3413.5 358.9 %all-gather.42.cloned.1.call-done = bf16[4096,2560]{1,0:T(8,128)(2,1)} async-done(((bf16[512,2560]{1,0:T(8,128)(2,1)}), bf16[4096,2560]{1,0:T(8,128)(2,1)}) %all-gather.42.cloned.1.call-update) | async-done | bytes 20971536 | tf_op jit(solution)/shard_map/all_gather | solution.py:273
  3802.3 41.8 %all-reduce.10 = (f32[2560]{0:T(1024)S(1)}, f32[2560]{0:T(1024)S(1)}) all-reduce(f32[2560]{0:T(1024)S(1)} %get-tuple-element.72, f32[2560]{0:T(1024)S(1)} %copy-done.51), channel_id=3, replica_groups=mesh['dp'=4,'seq'=8] {'dp','seq'}, use_global_device_ids=true, to_apply=%region_13.14.clone | all-reduce | flops 5120 | bytes 40960
  3906.0 33.1 reduce-scatter.7.cloned.1.call-done
  (332 shorter events, 846.4 us)
Async XLA Ops:
  7.2 70.7 %all-gather.18.cloned.1.call-start = ((), (), s32[]{:S(2)}) async-start(), calls=%async_computation.8 | async-start | bytes 3686400 | tf_op jit(solution)/shard_map/all_gather | solution.py:101
  7.9 132.7 %all-gather.24.cloned.1.call-start = ((), (), s32[]{:S(2)}) async-start(), calls=%async_computation.11 | async-start | bytes 3686400 | tf_op jit(solution)/shard_map/all_gather | solution.py:103
  8.7 275.1 %all-gather.30.cloned.1.call-start = ((), (), s32[]{:S(2)}) async-start(), calls=%async_computation.14 | async-start | bytes 11059200 | tf_op jit(solution)/shard_map/all_gather | solution.py:105
  9.4 416.8 %all-gather.34.cloned.1.call-start = ((), (), s32[]{:S(2)}) async-start(), calls=%async_computation.16 | async-start | bytes 11059200 | tf_op jit(solution)/shard_map/all_gather | solution.py:106
  10.0 558.7 %all-gather.28.cloned.1.call-start = ((), (), s32[]{:S(2)}) async-start(), calls=%async_computation.13 | async-start | bytes 11059200 | tf_op jit(solution)/shard_map/all_gather | solution.py:104
  10.6 593.0 %all-gather.22.cloned.1.call-start = ((), (), s32[]{:S(2)}) async-start(), calls=%async_computation.10 | async-start | bytes 3276800 | tf_op jit(solution)/shard_map/all_gather | solution.py:112
  47.6 632.8 %all-gather.20.cloned.1.call-start = ((), (), s32[]{:S(2)}) async-start(), calls=%async_computation.9 | async-start | bytes 16384000 | tf_op jit(solution)/shard_map/all_gather | solution.py:111
  77.9 699.1 %all-gather.26.cloned.1.call-start = ((), (), s32[]{:S(2)}) async-start(), calls=%async_computation.12 | async-start | bytes 16384000 | tf_op jit(solution)/shard_map/all_gather | solution.py:113
  140.6 1548.6 %all-gather.32.cloned.1.call-start = ((), (), s32[]{:S(2)}) async-start(), calls=%async_computation.15 | async-start | bytes 49152000 | tf_op jit(solution)/shard_map/all_gather | solution.py:115
  283.7 1434.7 %all-gather.36.cloned.1.call-start = ((), (), s32[]{:S(2)}) async-start(), calls=%async_computation.17 | async-start | bytes 49152000 | tf_op jit(solution)/shard_map/all_gather | solution.py:116
  426.3 1359.7 %all-gather.38.cloned.1.call-start = ((), (), s32[]{:S(2)}) async-start(), calls=%async_computation.18 | async-start | bytes 49152000 | tf_op jit(solution)/shard_map/all_gather | solution.py:193
  568.7 2066.7 %all-gather.44.cloned.1.call-start = ((), (), s32[]{:S(2)}) async-start(), calls=%async_computation.21 | async-start | bytes 23592960 | tf_op jit(solution)/shard_map/all_gather | solution.py:205
  625.4 15.3 collective-permute-start
  641.6 14.6 collective-permute-start
  796.9 2080.3 %all-gather.46.cloned.1.call-start = ((), (), s32[]{:S(2)}) async-start(), calls=%async_computation.22 | async-start | bytes 23592960 | tf_op jit(solution)/shard_map/all_gather | solution.py:206
  797.6 2559.8 %all-gather.40.cloned.1.call-start = ((), (), s32[]{:S(2)}) async-start(), calls=%async_computation.19 | async-start | bytes 23592960 | tf_op jit(solution)/shard_map/all_gather | solution.py:272
  811.5 400.2 %collective-permute-start.2 = (bf16[640,7680]{1,0:T(8,128)(2,1)}, bf16[640,7680]{1,0:T(8,128)(2,1)}, u32[]{:S(2)}, u32[]{:S(2)}) collective-permute-start(bf16[640,7680]{1,0:T(8,128)(2,1)} %copy.91), channel_id=1, source_target_pairs={{0,8},{8,16},{16,24},{24,0},{1,9},{9,17},{17,25},{25,1},{2,10},{10... | collective-permute-start | bytes 29491208 | tf_op jit(solution)/shard_map/ppermute | solution.py:30
  811.8 399.9 %collective-permute-start.4 = (bf16[640,7680]{1,0:T(8,128)(2,1)}, bf16[640,7680]{1,0:T(8,128)(2,1)}, u32[]{:S(2)}, u32[]{:S(2)}) collective-permute-start(bf16[640,7680]{1,0:T(8,128)(2,1)} %copy.91), channel_id=1, source_target_pairs={{8,0},{16,8},{24,16},{0,24},{9,1},{17,9},{25,17},{1,25},{10,2},{18... | collective-permute-start | bytes 29491208 | tf_op jit(solution)/shard_map/ppermute | solution.py:36
  1211.7 318.1 %collective-permute-start.3 = (bf16[640,7680]{1,0:T(8,128)(2,1)}, bf16[640,7680]{1,0:T(8,128)(2,1)}, u32[]{:S(2)}, u32[]{:S(2)}) collective-permute-start(bf16[640,7680]{1,0:T(8,128)(2,1)} %collective-permute-done.2), channel_id=1, source_target_pairs={{0,8},{8,16},{16,24},{24,0},{1,9},{9,17},{17,25},{25,1},{2,10},{10... | collective-permute-start | bytes 29491208 | tf_op jit(solution)/shard_map/ppermute | solution.py:30
  1769.0 261.4 %all-to-all-start.5 = ((bf16[512,8,960]{0,2,1:T(8,128)(2,1)}), bf16[512,8,960]{0,2,1:T(8,128)(2,1)}, u32[]{:S(2)}, u32[]{:S(2)}) async-start(bf16[512,8,960]{0,2,1:T(8,128)(2,1)} %bitcast.119), calls=%async_computation.5 | async-start | bytes 15728640 | tf_op jit(solution)/shard_map/all_to_all | solution.py:211
  2030.4 284.3 %all-to-all-start.4 = ((bf16[512,8,960]{0,2,1:T(8,128)(2,1)}), bf16[512,8,960]{0,2,1:T(8,128)(2,1)}, u32[]{:S(2)}, u32[]{:S(2)}) async-start(bf16[512,8,960]{0,2,1:T(8,128)(2,1)} %bitcast.117), calls=%async_computation.4 | async-start | bytes 15728640 | tf_op jit(solution)/shard_map/all_to_all | solution.py:210
  2076.7 1695.7 %all-gather.42.cloned.1.call-start = ((), (), s32[]{:S(2)}) async-start(), calls=%async_computation.20 | async-start | bytes 23592960 | tf_op jit(solution)/shard_map/all_gather | solution.py:273
  2314.7 245.8 %all-to-all-start.3 = ((bf16[512,8,960]{0,2,1:T(8,128)(2,1)}), bf16[512,8,960]{0,2,1:T(8,128)(2,1)}, u32[]{:S(2)}, u32[]{:S(2)}) async-start(bf16[512,8,960]{0,2,1:T(8,128)(2,1)} %bitcast.118), calls=%async_computation.3 | async-start | bytes 15728640 | tf_op jit(solution)/shard_map/all_to_all | solution.py:209
  2560.4 726.9 %all-to-all-start.2 = ((bf16[512,8,320]{0,2,1:T(8,128)(2,1)}), bf16[512,8,320]{0,2,1:T(8,128)(2,1)}, u32[]{:S(2)}, u32[]{:S(2)}) async-start(bf16[512,8,320]{0,2,1:T(8,128)(2,1)} %bitcast.126), calls=%async_computation.2 | async-start | bytes 5242880 | tf_op jit(solution)/shard_map/all_to_all | solution.py:278
  2627.8 1266.1 %reduce-scatter.9.cloned.1.call-start = ((), (), s32[]{:S(2)}) async-start(), calls=%async_computation.24 | async-start | bytes 18841600
  3071.7 73.7 %collective-permute-start.1 = (bf16[512,512]{1,0:T(8,128)(2,1)S(1)}, bf16[512,512]{1,0:T(8,128)(2,1)S(1)}, u32[]{:S(2)}, u32[]{:S(2)}) collective-permute-start(bf16[512,512]{1,0:T(8,128)(2,1)S(1)} %fusion.108), channel_id=1, source_target_pairs={{1,0},{2,1},{3,2},{4,3},{5,4},{6,5},{7,6},{9,8},{10,9},{11,10},{12... | collective-permute-start | bytes 1572872 | tf_op jit(solution)/shard_map/while/body/eval_jaxpr/ppermute | solution.py:48
  3147.1 41.8 %collective-permute-start.1 = (bf16[512,512]{1,0:T(8,128)(2,1)S(1)}, bf16[512,512]{1,0:T(8,128)(2,1)S(1)}, u32[]{:S(2)}, u32[]{:S(2)}) collective-permute-start(bf16[512,512]{1,0:T(8,128)(2,1)S(1)} %fusion.108), channel_id=1, source_target_pairs={{1,0},{2,1},{3,2},{4,3},{5,4},{6,5},{7,6},{9,8},{10,9},{11,10},{12... | collective-permute-start | bytes 1572872 | tf_op jit(solution)/shard_map/while/body/eval_jaxpr/ppermute | solution.py:48
  3190.5 35.3 collective-permute-start.1
  3227.5 39.8 %collective-permute-start.1 = (bf16[512,512]{1,0:T(8,128)(2,1)S(1)}, bf16[512,512]{1,0:T(8,128)(2,1)S(1)}, u32[]{:S(2)}, u32[]{:S(2)}) collective-permute-start(bf16[512,512]{1,0:T(8,128)(2,1)S(1)} %fusion.108), channel_id=1, source_target_pairs={{1,0},{2,1},{3,2},{4,3},{5,4},{6,5},{7,6},{9,8},{10,9},{11,10},{12... | collective-permute-start | bytes 1572872 | tf_op jit(solution)/shard_map/while/body/eval_jaxpr/ppermute | solution.py:48
  3287.3 21.7 all-to-all-start.1
  3309.0 91.6 %all-to-all-start = ((bf16[512,8,320]{0,2,1:T(8,128)(2,1)}), bf16[512,8,320]{0,2,1:T(8,128)(2,1)S(1)}, u32[]{:S(2)}, u32[]{:S(2)}) async-start(bf16[512,8,320]{0,2,1:T(8,128)(2,1)} %bitcast.129), calls=%async_computation | async-start | bytes 5242880 | tf_op jit(solution)/shard_map/all_to_all | solution.py:276
  3328.1 610.9 %reduce-scatter.7.cloned.1.call-start = ((), (), s32[]{:S(2)}) async-start(), calls=%async_computation.23 | async-start | bytes 4915200
  (66 other events, 2127.8 us)
Sparse Core Ops, SparseCore 0:
  10.2 67.6 all-gather.17
  80.1 60.4 all-gather.23
  142.8 140.8 all-gather.29
  285.8 140.3 all-gather.33
  428.2 140.3 all-gather.27
  570.1 23.6 all-gather.21
  595.4 84.9 all-gather.19
  682.0 84.9 all-gather.25
  768.5 421.8 all-gather.31
  1191.9 340.1 all-gather.35
  1533.7 235.5 all-gather.37
  1770.7 621.3 all-gather.43
  2393.7 483.4 all-gather.45
  2879.1 478.2 all-gather.39
  3358.8 413.5 all-gather.41
  3774.9 118.9 reduce-scatter.8
  3896.3 42.7 reduce-scatter.6
